TPU v7x, 512 devices: a whole 4x4x16 slice. The times are simulated.
512 devices in a mesh: gx: 8 (over y, core), gy: 16 (over z), lev: 4 (over x).
Axes of the slice: x: 4, y: 4, z: 16, core: 2. Of those that a mesh axis runs over, the one named last changes fastest.
Arguments:
- state: bfloat16 [1024, 128, 8, 512], P('gx', 'gy', 'lev'), may hold values from -6 to 6
- obs_col: int32 [4096], P('gx'), may hold values from 0 to 127
- obs_row: int32 [4096], P('gx'), may hold values from 0 to 127
- foot_off: int32 [4096, 8], P('gx'), may hold values from 0 to 84
- obs_lev: int32 [4096], P('gx'), may hold values from 0 to 7
- obs_val: float32 [4096], P('gx'), may hold values from -6 to 6
- obs_err: float32 [4096], P('gx'), may hold values from 0.5 to 2
- loc: bfloat16 [1024, 128, 512], P('gx', ('gy', 'lev')), may hold values from 0.099609375 to 1
Outputs:
- mean_out: float32 [1024, 128, 8], P('gx', ('gy', 'lev'))
- anom_out: bfloat16 [1024, 128, 8, 512], P('gx', ('gy', 'lev'))
All inputs are finite; a program needn't handle non-finite values.
Results may differ from a plain program's by a relative error of at most 0.009.
Values may be sent and summed in bfloat16 or wider, within the bound.
No kernel may reach another device: no remote copies, remote signals or barrier semaphores. Data moves between devices by JAX's collectives and lax.ppermute only.
A program may use at most 64 MiB of HBM per device.

v0:
```python
import functools

import jax, jax.numpy as jnp
from jax import lax
from jax.experimental import pallas as pl
from jax.experimental.pallas import tpu as pltpu
from jax.sharding import PartitionSpec as P

KF = 8
HW = 8
DY = 2
F32=jnp.float32
BF=jnp.bfloat16
HI=lax.Precision.HIGHEST
SUB=32
SUP=128

def mm(a,b,dims,prec=HI):
    return lax.dot_general(a,b,(dims,((),())),precision=prec,preferred_element_type=F32)
def mm3(a,b):
    hi=a.astype(BF)
    rest=a-hi.astype(F32)
    mid=rest.astype(BF)
    low=(rest-mid.astype(F32)).astype(BF)
    return mm(hi,b,NN,None)+(mm(mid,b,NN,None)+mm(low,b,NN,None))
NN=((1,),(0,)); NT=((1,),(1,)); TN=((0,),(0,))

def factor_block(R, off, sq):
    nv=SUB//8
    row=lax.broadcasted_iota(jnp.int32,(8,128),0)
    lane=lax.broadcasted_iota(jnp.int32,(8,128),1)
    C=[[jnp.broadcast_to(R[8*v:8*v+8, off+j:off+j+1],(8,128)) if v>=j//8 else None for v in range(nv)] for j in range(SUB)]
    X=[jnp.where(lane==row+8*v,1.0,0.0).astype(F32) for v in range(nv)]
    G=list(X)
    rs=[jnp.zeros((8,128),F32) for _ in range(nv)]
    def rowb(t,i):
        return jnp.broadcast_to(t[i:i+1,:],(8,128))
    for j in range(SUB):
        vj,ij=divmod(j,8)
        p=rowb(C[j][vj],ij)
        inv=1.0/p
        col=[C[j][v] if v>=vj else None for v in range(nv)]
        q=[None if c is None else c*inv for c in col]
        for k in range(j+1,SUB):
            vk,ik=divmod(k,8)
            ck=rowb(col[vk],ik)
            for v in range(vk,nv):
                C[k][v]=C[k][v]-q[v]*ck
        r=lax.rsqrt(p)
        below=row>ij
        qm=[None if t is None else t for t in q]
        qm[vj]=jnp.where(below,q[vj],0.0)
        rs[vj]=jnp.where(row==ij,r,rs[vj])
        sp=p*r
        xj=rowb(X[vj],ij)
        g=1.0/(sp+rowb(sq[vj],ij))
        gj=rowb(G[vj],ij)*g
        G[vj]=jnp.where(row==ij,gj,G[vj])
        gs=gj*sp
        for v in range(vj,nv):
            X[v]=X[v]-qm[v]*xj
            G[v]=G[v]-qm[v]*gs
    X=[X[v]*rs[v] for v in range(nv)]
    return jnp.concatenate(X,0)[:,:SUB], jnp.concatenate(G,0)[:,:SUB]

def solve_kernel(y_ref, innov_ref, errr_ref, errc_ref, z_ref, w_ref, A, U, Li, Gi):
    n=A.shape[0]
    M=y_ref.shape[1]
    y=y_ref[...]
    A[...]=mm(y,y,NT,None)*(1.0/(M-1))
    Li[...]=jnp.zeros_like(Li)
    Gi[...]=jnp.zeros_like(Gi)
    sup=n//SUP
    ii=lax.broadcasted_iota(jnp.int32,(SUP,SUP),0)
    jj=lax.broadcasted_iota(jnp.int32,(SUP,SUP),1)
    for s in range(sup):
        w0=s*SUP
        A[w0:w0+SUP,w0:w0+SUP]=A[w0:w0+SUP,w0:w0+SUP]+jnp.where(ii==jj,errr_ref[:,w0:w0+SUP],0.0)
    for s in range(sup):
        w0=s*SUP
        for t in range(SUP//SUB):
            k0=w0+t*SUB
            R=A[k0:k0+SUB,w0:n]
            if t:
                R=R-mm(U[w0:k0,k0:k0+SUB],U[w0:k0,w0:n],TN)
            sq=jnp.broadcast_to(jnp.sqrt(errc_ref[k0:k0+SUB,:]),(SUB,128))
            sq=[sq[8*v:8*v+8] for v in range(SUB//8)]
            x,g=factor_block(R,t*SUB,sq)
            U[k0:k0+SUB,w0:n]=mm(x,R,NN)
            Li[k0:k0+SUB,k0:k0+SUB]=x
            Gi[k0:k0+SUB,k0:k0+SUB]=g
        w1=w0+SUP
        if w1<n:
            A[w1:n,w1:n]=A[w1:n,w1:n]-mm(U[w0:w1,w1:n],U[w0:w1,w1:n],TN)
    for s in range(sup):
        w0=s*SUP
        L=U[w0:w0+SUP,w0:w0+SUP].T
        for B in (Li,Gi):
            T=B[w0:w0+SUP,w0:w0+SUP]
            size=SUB
            while size<SUP:
                mask=((ii//(2*size))==(jj//(2*size)))&((ii//size)>(jj//size))
                N=jnp.where(mask,L,0.0)
                T=T-mm(T,mm(N,T,NN),NN)
                size*=2
            B[w0:w0+SUP,w0:w0+SUP]=T
    size=SUP
    while size<n:
        for a0 in range(0,n,2*size):
            b0=a0+size; b1=b0+size
            for B in (Li,Gi):
                t=mm(U[a0:b0,b0:b1],B[a0:b0,a0:b0],TN)
                B[b0:b1,a0:b0]=-mm(B[b0:b1,b0:b1],t,NN)
        size*=2
    S=jnp.concatenate([mm3(Gi[s*SUP:(s+1)*SUP,:(s+1)*SUP],y_ref[:(s+1)*SUP,:]) for s in range(sup)],0)
    v=jnp.sum(Li[...]*innov_ref[...],axis=1,keepdims=True)
    w=jnp.sum(Li[...]*v,axis=0,keepdims=True)
    hi=w.astype(BF).astype(F32)
    mid=(w-hi).astype(BF).astype(F32)
    pick=lax.broadcasted_iota(jnp.int32,w_ref.shape,0)
    w_ref[...]=jnp.where(pick==0,hi,jnp.where(pick==1,mid,jnp.where(pick==2,w-hi-mid,0.0))).astype(BF)
    for s in range(sup):
        z_ref[s*SUP:(s+1)*SUP,:]=mm(Li[s*SUP:,s*SUP:(s+1)*SUP],S[s*SUP:],TN).astype(z_ref.dtype)

def solve(y, innov, err):
    n,M=y.shape
    return pl.pallas_call(solve_kernel,
        out_shape=(jax.ShapeDtypeStruct((n,M),BF),jax.ShapeDtypeStruct((16,n),BF)),
        in_specs=[pl.BlockSpec(memory_space=pltpu.VMEM)]*4,
        out_specs=(pl.BlockSpec(memory_space=pltpu.VMEM),)*2,
        scratch_shapes=[pltpu.VMEM((n,n),F32)]*4,
        compiler_params=pltpu.CompilerParams(vmem_limit_bytes=40<<20),
        cost_estimate=pl.CostEstimate(flops=6*10**9,bytes_accessed=2<<20,transcendentals=0),
    )(y, innov[None,:], err[None,:], err[:,None])


def split3(x):
    hi = lax.reduce_precision(x, 8, 7)
    mid = lax.reduce_precision(x - hi, 8, 7)
    return hi, mid, x - hi - mid


def pack(anom, mean):
    cols = jnp.stack(split3(mean), axis=-1)
    cols = jnp.pad(cols, [(0, 0)] * (cols.ndim - 1) + [(0, 125)])
    return jnp.concatenate([anom, cols], axis=-1).astype(BF)


def unpack_sum(parts, members):
    total = jnp.sum(parts.astype(F32), axis=0)
    return total[..., :members], jnp.sum(total[..., members:], axis=-1)


def swap(array, axis):
    return lax.all_to_all(array, axis, split_axis=0, concat_axis=0, tiled=True)


def hits_of(codes, base, lanes):
    col = lax.broadcasted_iota(jnp.int32, (codes[0].shape[0], lanes), 1) + base
    total = jnp.where(codes[0] == col, 1.0, 0.0)
    for code in codes[1:]:
        total = total + jnp.where(code == col, 1.0, 0.0)
    return total.astype(BF)


def inner_kernel(code_ref, rows_ref, out_ref, same_ref, codes):
    step = pl.program_id(0)

    @pl.when(step == 0)
    def _():
        for k in range(codes.shape[0]):
            codes[k] = jnp.broadcast_to(code_ref[:, k : k + 1], codes.shape[1:])
        out_ref[...] = jnp.zeros_like(out_ref)

    wide = rows_ref.shape[0]
    parts = [codes[k] for k in range(codes.shape[0])]
    select = jnp.concatenate([hits_of(parts, step * wide + c, 128) for c in range(0, wide, 128)], axis=1)
    out_ref[...] += jnp.dot(select, rows_ref[...], preferred_element_type=F32)


def inner(code, rows):
    n_obs, slots = code.shape
    total, members = rows.shape
    wide = 256
    return pl.pallas_call(
        inner_kernel,
        out_shape=(
            jax.ShapeDtypeStruct((n_obs, members), F32),
            jax.ShapeDtypeStruct(rows.shape, rows.dtype),
        ),
        grid=(total // wide,),
        in_specs=[
            pl.BlockSpec((n_obs, slots), lambda i: (0, 0)),
            pl.BlockSpec((wide, members), lambda i: (i, 0)),
        ],
        out_specs=(
            pl.BlockSpec((n_obs, members), lambda i: (0, 0)),
            pl.BlockSpec(memory_space=pl.ANY),
        ),
        input_output_aliases={1: 1},
        scratch_shapes=[pltpu.VMEM((slots, n_obs, 128), jnp.int32)],
        cost_estimate=pl.CostEstimate(flops=2 * 10**9, bytes_accessed=2 << 20, transcendentals=0),
    )(code, rows)


def edge_kernel(first, code_ref, before_ref, after_ref, inner_ref, out_ref):
    n_obs, slots = code_ref.shape
    members = inner_ref.shape[1]
    wide = before_ref.shape[0]
    codes = [jnp.broadcast_to(code_ref[:, k : k + 1], (n_obs, wide)) for k in range(slots)]
    total = inner_ref[...]
    total += jnp.dot(hits_of(codes, first, wide), before_ref[...], preferred_element_type=F32)
    total += jnp.dot(hits_of(codes, first + wide, wide), after_ref[...], preferred_element_type=F32)
    total = total * (1.0 / KF)
    mean = jnp.sum(total, axis=1, keepdims=True) * (1.0 / members)
    out_ref[:, :members] = (total - mean).astype(BF)
    hi = mean.astype(BF).astype(F32)
    mid = (mean - hi).astype(BF).astype(F32)
    lane = lax.broadcasted_iota(jnp.int32, (n_obs, 128), 1)
    cols = jnp.where(lane == 0, hi, jnp.where(lane == 1, mid, jnp.where(lane == 2, mean - hi - mid, 0.0)))
    out_ref[:, members:] = cols.astype(BF)


def with_edges(first, code, before, after, part):
    n_obs, members = part.shape
    return pl.pallas_call(
        functools.partial(edge_kernel, first),
        out_shape=jax.ShapeDtypeStruct((n_obs, members + 128), BF),
        in_specs=[pl.BlockSpec(memory_space=pltpu.VMEM)] * 4,
        out_specs=pl.BlockSpec(memory_space=pltpu.VMEM),
        cost_estimate=pl.CostEstimate(flops=10**9, bytes_accessed=1 << 20, transcendentals=0),
    )(code, before, after, part)


def observe(grid, obs_col, obs_row, foot_off, obs_lev, ny_total):
    ny, nl, nx, members = grid.shape
    span = 2 * DY + 1
    x = obs_col[:, None] + foot_off // span - HW
    y = jnp.clip(obs_row[:, None] + foot_off % span - DY, 0, ny_total - 1) - lax.axis_index("gy") * ny
    lv = obs_lev[:, None] - lax.axis_index("lev") * nl
    inside = (y >= 0) & (y < ny) & (lv >= 0) & (lv < nl)
    place = y * nl + lv
    edge = ny * nl * HW
    total = ny * nl * nx
    low = total + place * HW + x + HW
    high = total + edge + place * HW + x - nx
    code = jnp.where(x < 0, low, jnp.where(x >= nx, high, place * nx + x))
    code = jnp.where(inside, code, -1)
    size = lax.axis_size("gx")
    up = [(i, (i + 1) % size) for i in range(size)]
    down = [(j, i) for i, j in up]
    before = lax.ppermute(grid[:, :, nx - HW :], "gx", up).reshape(edge, members)
    after = lax.ppermute(grid[:, :, :HW], "gx", down).reshape(edge, members)
    part, rows = inner(code, grid.reshape(total, members))
    return with_edges(total, code, before, after, part), rows


def share(msg):
    members = msg.shape[1] - 128
    for axis in ("lev", "gy"):
        size = lax.axis_size(axis)
        got = swap(msg.reshape(size, msg.shape[0] // size, msg.shape[1]), axis)
        msg = pack(*unpack_sum(got, members))
    size = lax.axis_size("gy")
    msg = swap(jnp.broadcast_to(msg[None], (size,) + msg.shape), "gy").reshape(-1, msg.shape[1])
    msg = lax.all_gather(msg, "lev", axis=0, tiled=True)
    return msg[:, :members], jnp.sum(msg[:, members : members + 3].astype(F32), axis=1)


def update_kernel(got_ref, loc_ref, y_ref, z_ref, w_ref, out_ref, mean_ref):
    nx = got_ref.shape[3]
    members = got_ref.shape[4]
    nl = got_ref.shape[2]
    levels = got_ref.shape[0] * nl
    rows = nx * levels
    ii = lax.broadcasted_iota(jnp.int32, (rows, rows), 0)
    jj = lax.broadcasted_iota(jnp.int32, (rows, rows), 1)
    order = jnp.where(jj == (ii % levels) * nx + ii // levels, 1.0, 0.0).astype(BF)
    for y in range(got_ref.shape[1]):
        block = jnp.concatenate([got_ref[lv // nl, y, lv % nl] for lv in range(levels)], axis=0)
        block = jnp.dot(order, block, preferred_element_type=F32)
        xbar = jnp.sum(block, axis=1, keepdims=True) * (1.0 / members)
        anom = (block - xbar).astype(BF)
        cross = mm(anom, y_ref[...], NT, None) * (1.0 / (members - 1))
        weight = loc_ref[y].astype(F32)
        weight = jnp.broadcast_to(weight[:, None, :], (nx, levels, weight.shape[1])).reshape(rows, weight.shape[1])
        gain = (cross * weight).astype(BF)
        result = anom.astype(F32) - jnp.dot(gain, z_ref[...], preferred_element_type=F32)
        out_ref[:, y] = result.reshape(nx, levels, members).astype(BF)
        shift = jnp.sum(mm(gain, w_ref[...], NT, None), axis=1, keepdims=True)
        mean = jnp.where(ii == jj, xbar + shift, 0.0)
        mean_ref[0, y : y + 1] = jnp.sum(mean, axis=0, keepdims=True)


def update(got, loc, ybf, zmat, wrows):
    parts, ny, nl, nx, members = got.shape
    n_obs = ybf.shape[0]
    levels = parts * nl
    wide = 16
    whole = lambda i: (0, 0)
    out, mean = pl.pallas_call(
        update_kernel,
        out_shape=(
            jax.ShapeDtypeStruct((nx, ny, levels, members), BF),
            jax.ShapeDtypeStruct((nx // wide, ny, wide * levels), F32),
        ),
        grid=(nx // wide,),
        in_specs=[
            pl.BlockSpec((parts, ny, nl, wide, members), lambda i: (0, 0, 0, i, 0)),
            pl.BlockSpec((ny, wide, n_obs), lambda i: (0, i, 0)),
            pl.BlockSpec(ybf.shape, whole),
            pl.BlockSpec(zmat.shape, whole),
            pl.BlockSpec(wrows.shape, whole),
        ],
        out_specs=(
            pl.BlockSpec((wide, ny, levels, members), lambda i: (i, 0, 0, 0)),
            pl.BlockSpec((1, ny, wide * levels), lambda i: (i, 0, 0)),
        ),
        cost_estimate=pl.CostEstimate(flops=3 * 10**9, bytes_accessed=5 << 20, transcendentals=0),
    )(got, loc, ybf, zmat, wrows)
    mean = mean.reshape(nx // wide, ny, wide, levels).transpose(0, 2, 1, 3).reshape(nx, ny, levels)
    return mean, out


def local(state, obs_col, obs_row, foot_off, obs_lev, obs_val, obs_err, loc):
    nx, ny, nl, members = state.shape
    grid = lax.optimization_barrier(jnp.transpose(state, (1, 2, 0, 3)))
    msg, grid = observe(grid, obs_col, obs_row, foot_off, obs_lev, ny * lax.axis_size("gy"))
    ybf, hbar = share(msg)
    size = lax.axis_size("lev")
    grid, ybf, hbar = lax.optimization_barrier((grid, ybf, hbar))
    got = swap(grid.reshape(size, ny // size, nl, nx, members), "lev")
    zmat, wrows = solve(ybf, obs_val - hbar, obs_err)
    return update(got, jnp.transpose(loc, (1, 0, 2)), ybf, zmat, wrows)


def solution(mesh):
    return jax.shard_map(
        local,
        mesh=mesh,
        in_specs=(
            P("gx", "gy", "lev", None),
            P("gx"),
            P("gx"),
            P("gx", None),
            P("gx"),
            P("gx"),
            P("gx"),
            P("gx", ("gy", "lev"), None),
        ),
        out_specs=(P("gx", ("gy", "lev"), None), P("gx", ("gy", "lev"), None, None)),
        check_vma=False,
    )
```

profile of v0, /device:TPU:10, one launch (start us, length us, event | category | flops | bytes accessed | tf_op | source)
XLA Modules:
  0.0 152.2 jit_solution(7256563441322127646)
XLA Ops:
  0.6 1.2 fusion.13
  1.8 1.7 %collective-permute-start.1 = (bf16[8,2,8,512]{3,1,0,2:T(2,128)(2,1)S(1)}, bf16[8,2,8,512]{3,1,0,2:T(2,128)(2,1)S(1)}, u32[]{:S(2)}, u32[]{:S(2)}) collective-permute-start(bf16[8,2,8,512]{3,1,0,2:T(2,128)(2,1)S(1)} %get-tuple-element.28), channel_id=1, source_target_pairs={{64,0},{128,64},{192,128},{256,192},{320,256},{384,320},{448,384},... | collective-permute-start | bytes 393224 | tf_op jit(solution)/shard_map/ppermute | solution.py:253
  3.6 0.7 broadcast_divide_fusion
  4.3 0.8 copy.55
  5.2 4.1 %copy.66 = bf16[8,2,128,512]{3,2,1,0:T(8,128)(2,1)} copy(bf16[8,2,128,512]{3,1,0,2:T(2,128)(2,1)} %bitcast.34) | data formatting | bytes 4194304 | tf_op jit(solution)/shard_map/optimization_barrier | solution.py:327
  9.6 1.4 select_select_fusion.code_ref
  11.0 8.3 %shard_map.95 = (f32[512,512]{1,0:T(8,128)}, bf16[2048,512]{1,0:T(8,128)(2,1)}) custom-call(s32[512,8]{1,0:T(8,128)} %select_select_fusion.code_ref, bf16[2048,512]{1,0:T(8,128)(2,1)} %bitcast.1.rows_ref), custom_call_target="tpu_custom_call", output_to_operand_aliasing={{1}: (1, {})} | custom-call | flops 2000000000 | bytes 2097152 | tf_op jit(solution)/shard_map/pallas_call | solution.py:185
  19.2 0.7 copy.67
  20.0 0.7 copy.68
  20.7 3.6 %shard_map.96 = bf16[512,640]{1,0:T(8,128)(2,1)} custom-call(s32[512,8]{1,0:T(8,128)} %select_select_fusion.code_ref, bf16[128,512]{1,0:T(8,128)(2,1)} %bitcast.39, bf16[128,512]{1,0:T(8,128)(2,1)} %bitcast.40, f32[512,512]{1,0:T(8,128)} %get-tuple-element.12.inner_ref), custom_call_target="tpu_custom_call" | custom-call | flops 1000000000 | bytes 1048576 | tf_op jit(solution)/shard_map/pallas_call | solution.py:226
  24.3 14.4 %all_to_all.20 = bf16[4,128,640]{2,1,0:T(8,128)(2,1)S(1)} all-to-all(bf16[4,128,640]{2,1,0:T(8,128)(2,1)} %bitcast.35), channel_id=1, replica_groups=mesh['gx'=8,'gy'=16,'lev'=4] {'lev'}, dimensions={0} | all-to-all | bytes 1310720 | tf_op jit(solution)/shard_map/all_to_all | solution.py:155
  39.1 29.7 %all_to_all.21 = bf16[16,8,640]{2,1,0:T(8,128)(2,1)S(1)} all-to-all(bf16[16,8,640]{2,1,0:T(8,128)(2,1)S(1)} %pad_maximum_fusion), channel_id=1, replica_groups=mesh['gx'=8,'gy'=16,'lev'=4] {'gy'}, dimensions={0} | all-to-all | bytes 327680 | tf_op jit(solution)/shard_map/all_to_all | solution.py:155
  69.2 18.6 %all_to_all.22 = bf16[16,8,640]{2,1,0:T(8,128)(2,1)S(1)} all-to-all(bf16[16,8,640]{2,1,0:T(8,128)(2,1)S(1)} %broadcast_in_dim.10), channel_id=1, replica_groups=mesh['gx'=8,'gy'=16,'lev'=4] {'gy'}, dimensions={0} | all-to-all | bytes 327680 | tf_op jit(solution)/shard_map/all_to_all | solution.py:155
  87.8 13.3 %all_gather.3 = bf16[512,640]{1,0:T(8,128)(2,1)S(1)} all-gather(bf16[128,640]{1,0:T(8,128)(2,1)S(1)} %bitcast.36), channel_id=1, replica_groups=mesh['gx'=8,'gy'=16,'lev'=4] {'lev'}, dimensions={0}, use_global_device_ids=true | all-gather | bytes 819200 | tf_op jit(solution)/shard_map/all_gather | solution.py:266
  101.3 5.8 %all-to-all-start.3 = ((bf16[4,2,2,128,512]{4,3,2,1,0:T(8,128)(2,1)}), bf16[4,2,2,128,512]{4,3,2,1,0:T(8,128)(2,1)S(1)}, u32[]{:S(2)}, u32[]{:S(2)}) async-start(bf16[4,2,2,128,512]{4,3,2,1,0:T(8,128)(2,1)} %bitcast.10), calls=%async_computation.3 | async-start | bytes 4194304 | tf_op jit(solution)/shard_map/all_to_all | solution.py:155
  107.1 0.1 copy.73.errc_ref
  107.2 0.7 copy.78
  108.0 26.9 %shard_map.97 = (bf16[512,512]{1,0:T(8,128)(2,1)S(1)}, bf16[16,512]{1,0:T(8,128)(2,1)S(1)}) custom-call(bf16[512,512]{1,0:T(8,128)(2,1)S(1)} %slice.40.y_ref, f32[1,512]{1,0:T(1,128)S(1)} %bitcast.32, f32[1,512]{1,0:T(1,128)S(1)} %bitcast.31, f32[512,1]{1,0:T(8,128)S(1)} %copy.73.errc_ref), custom_call_target="tpu_custom_call" | custom-call | flops 6000000000 | bytes 2097152 | tf_op jit(solution)/shard_map/pallas_call | solution.py:127
  134.9 0.8 copy-done.2
  135.7 0.6 copy-done.3
  136.3 1.3 copy-done.4
  137.6 13.1 %shard_map.98 = (bf16[128,2,8,512]{3,2,1,0:T(8,128)(2,1)}, f32[8,2,128]{2,1,0:T(2,128)}) custom-call(bf16[4,2,2,128,512]{4,3,2,1,0:T(8,128)(2,1)} %copy-done.4, bf16[2,128,512]{2,1,0:T(8,128)(2,1)} %bitcast.38, bf16[512,512]{1,0:T(8,128)(2,1)} %copy-done, bf16[512,512]{1,0:T(8,128)(2,1)} %copy-done.2, bf16[16,512]{1,0:T(8,128)(2,1)} %copy-done.3), custom_call_target="tpu_custom_call" | custom-call | flops 3000000000 | bytes 5242880 | tf_op jit(solution)/shard_map/pallas_call | solution.py:301
  150.7 0.7 copy.74
  151.5 0.7 copy.75
  (45 shorter events, 1.3 us)
Async XLA Ops:
  1.8 17.4 %collective-permute-start = (bf16[8,2,8,512]{3,1,0,2:T(2,128)(2,1)S(1)}, bf16[8,2,8,512]{3,1,0,2:T(2,128)(2,1)S(1)}, u32[]{:S(2)}, u32[]{:S(2)}) collective-permute-start(bf16[8,2,8,512]{3,1,0,2:T(2,128)(2,1)S(1)} %get-tuple-element.29), channel_id=1, source_target_pairs={{0,64},{64,128},{128,192},{192,256},{256,320},{320,384},{384,448},... | collective-permute-start | bytes 393224 | tf_op jit(solution)/shard_map/ppermute | solution.py:252
  1.8 18.2 %collective-permute-start.1 = (bf16[8,2,8,512]{3,1,0,2:T(2,128)(2,1)S(1)}, bf16[8,2,8,512]{3,1,0,2:T(2,128)(2,1)S(1)}, u32[]{:S(2)}, u32[]{:S(2)}) collective-permute-start(bf16[8,2,8,512]{3,1,0,2:T(2,128)(2,1)S(1)} %get-tuple-element.28), channel_id=1, source_target_pairs={{64,0},{128,64},{192,128},{256,192},{320,256},{384,320},{448,384},... | collective-permute-start | bytes 393224 | tf_op jit(solution)/shard_map/ppermute | solution.py:253
  5.1 4.1 %copy-start.9 = (s32[512]{0:T(512)S(1)}, s32[512]{0:T(512)}, u32[]{:S(2)}) copy-start(s32[512]{0:T(512)} %param.12) | copy-start | bytes 6148
  5.1 4.4 %copy-start.6 = (s32[512]{0:T(512)S(1)}, s32[512]{0:T(512)}, u32[]{:S(2)}) copy-start(s32[512]{0:T(512)} %param.9) | copy-start | bytes 6148
  5.2 4.4 %copy-start.7 = (s32[512]{0:T(512)S(1)}, s32[512]{0:T(512)}, u32[]{:S(2)}) copy-start(s32[512]{0:T(512)} %param.10) | copy-start | bytes 6148
  101.1 6.9 %copy-start = (bf16[512,512]{1,0:T(8,128)(2,1)}, bf16[512,512]{1,0:T(8,128)(2,1)S(1)}, u32[]{:S(2)}) copy-start(bf16[512,512]{1,0:T(8,128)(2,1)S(1)} %slice.40.y_ref) | copy-start | bytes 1572868
  101.3 5.8 %copy-start.1 = (f32[512]{0:T(512)S(1)}, f32[512]{0:T(512)}, u32[]{:S(2)}) copy-start(f32[512]{0:T(512)} %param.14) | copy-start | bytes 6148
  101.3 6.0 %copy-start.5 = (bf16[128,2,512]{2,1,0:T(2,128)(2,1)S(1)}, bf16[128,2,512]{2,1,0:T(2,128)(2,1)}, u32[]{:S(2)}) copy-start(bf16[128,2,512]{2,1,0:T(2,128)(2,1)} %param.15) | copy-start | bytes 786436
  101.3 6.7 %copy-start.8 = (f32[512]{0:T(512)S(1)}, f32[512]{0:T(512)}, u32[]{:S(2)}) copy-start(f32[512]{0:T(512)} %param.13) | copy-start | bytes 6148
  101.3 35.0 %all-to-all-start.3 = ((bf16[4,2,2,128,512]{4,3,2,1,0:T(8,128)(2,1)}), bf16[4,2,2,128,512]{4,3,2,1,0:T(8,128)(2,1)S(1)}, u32[]{:S(2)}, u32[]{:S(2)}) async-start(bf16[4,2,2,128,512]{4,3,2,1,0:T(8,128)(2,1)} %bitcast.10), calls=%async_computation.3 | async-start | bytes 4194304 | tf_op jit(solution)/shard_map/all_to_all | solution.py:155
  134.9 0.8 copy-start.2
  135.7 0.6 copy-start.3
  136.3 1.3 copy-start.4
where the time goes:
time: 153 us; the launch traced here: 152 us
  blocking collectives  76 us (50%)
  Pallas kernels  51.9 us (34%)
  local copies, waits for them, and re-layouts  13.2 us (9%)
  starting transfers between devices  7.54 us (5%)
  other arithmetic  2.72 us (2%)
    all_to_all x3, blocking collectives, swap(): return lax.all_to_all(array, axis, split_axis=0, concat_axis=0, tiled=True)  62.7 us
    pallas_call x1, Pallas kernels, solve(): pl.pallas_call(solve_kernel, out_shape=(jax.ShapeDtypeStruct((n, M), BF),...  26.9 us
    all_gather x1, blocking collectives, share(): msg = lax.all_gather(msg, 'lev', axis=0, tiled=True)  13.3 us
    pallas_call x1, Pallas kernels, update(): pl.pallas_call(update_kernel, out_shape=(jax.ShapeDtypeStruct((nx, ny, le...  13.1 us
    pallas_call x1, Pallas kernels, inner(): pl.pallas_call(inner_kernel, out_shape=(jax.ShapeDtypeStruct((n_obs, memb...  8.27 us
    all_to_all x1, starting transfers between devices, swap(): return lax.all_to_all(array, axis, split_axis=0, concat_axis=0, tiled=True)  5.79 us
    unnamed x24, local copies, waits for them, and re-layouts  5.15 us
    optimization_barrier x1, local copies, waits for them, and re-layouts, local(): grid = lax.optimization_barrier(jnp.transpose(state, (1, 2, 0, 3)))  4.08 us
  transfers between devices with their start and end apart: 3, of which 0 were waited for; matrix products, arithmetic and copies ran while one was open for 6% of the time, Pallas kernels for 23%

commit v1 on v0

--- a/solution.py
+++ b/solution.py
@@ -17,12 +17,9 @@
 
 def mm(a,b,dims,prec=HI):
     return lax.dot_general(a,b,(dims,((),())),precision=prec,preferred_element_type=F32)
-def mm3(a,b):
+def halves(a):
     hi=a.astype(BF)
-    rest=a-hi.astype(F32)
-    mid=rest.astype(BF)
-    low=(rest-mid.astype(F32)).astype(BF)
-    return mm(hi,b,NN,None)+(mm(mid,b,NN,None)+mm(low,b,NN,None))
+    return hi,(a-hi.astype(F32)).astype(BF)
 NN=((1,),(0,)); NT=((1,),(1,)); TN=((0,),(0,))
 
 def factor_block(R, off, sq):
@@ -112,7 +109,13 @@
                 t=mm(U[a0:b0,b0:b1],B[a0:b0,a0:b0],TN)
                 B[b0:b1,a0:b0]=-mm(B[b0:b1,b0:b1],t,NN)
         size*=2
-    S=jnp.concatenate([mm3(Gi[s*SUP:(s+1)*SUP,:(s+1)*SUP],y_ref[:(s+1)*SUP,:]) for s in range(sup)],0)
+    gh,gl=halves(Gi[...])
+    S=[]
+    for s in range(sup):
+        r,k=slice(s*SUP,(s+1)*SUP),(s+1)*SUP
+        S.append(mm(gh[r,:k],y[:k],NN,None)+mm(gl[r,:k],y[:k],NN,None))
+    sh,sl=halves(jnp.concatenate(S,0))
+    lh,ll=halves(Li[...].T)
     v=jnp.sum(Li[...]*innov_ref[...],axis=1,keepdims=True)
     w=jnp.sum(Li[...]*v,axis=0,keepdims=True)
     hi=w.astype(BF).astype(F32)
@@ -120,7 +123,9 @@
     pick=lax.broadcasted_iota(jnp.int32,w_ref.shape,0)
     w_ref[...]=jnp.where(pick==0,hi,jnp.where(pick==1,mid,jnp.where(pick==2,w-hi-mid,0.0))).astype(BF)
     for s in range(sup):
-        z_ref[s*SUP:(s+1)*SUP,:]=mm(Li[s*SUP:,s*SUP:(s+1)*SUP],S[s*SUP:],TN).astype(z_ref.dtype)
+        r,k=slice(s*SUP,(s+1)*SUP),s*SUP
+        z=mm(lh[r,k:],sh[k:],NN,None)+(mm(lh[r,k:],sl[k:],NN,None)+mm(ll[r,k:],sh[k:],NN,None))
+        z_ref[r,:]=z.astype(z_ref.dtype)
 
 def solve(y, innov, err):
     n,M=y.shape
@@ -129,7 +134,7 @@
         in_specs=[pl.BlockSpec(memory_space=pltpu.VMEM)]*4,
         out_specs=(pl.BlockSpec(memory_space=pltpu.VMEM),)*2,
         scratch_shapes=[pltpu.VMEM((n,n),F32)]*4,
-        compiler_params=pltpu.CompilerParams(vmem_limit_bytes=40<<20),
+        compiler_params=pltpu.CompilerParams(vmem_limit_bytes=24<<20),
         cost_estimate=pl.CostEstimate(flops=6*10**9,bytes_accessed=2<<20,transcendentals=0),
     )(y, innov[None,:], err[None,:], err[:,None])
 
@@ -163,54 +168,78 @@
     return total.astype(BF)
 
 
-def inner_kernel(code_ref, rows_ref, out_ref, same_ref, codes):
+def codes_of(ny_total, ny, nl, nx, col_ref, row_ref, lev_ref, foot_ref):
+    foot = foot_ref[...]
+    shift_x = lax.shift_right_logical(foot * 205, 10)
+    shift_y = foot - (2 * DY + 1) * shift_x
+    x = col_ref[...] + shift_x - HW
+    y = jnp.clip(row_ref[...] + shift_y - DY, 0, ny_total - 1) - lax.axis_index("gy") * ny
+    lv = lev_ref[...] - lax.axis_index("lev") * nl
+    inside = (y >= 0) & (y < ny) & (lv >= 0) & (lv < nl)
+    place = y * nl + lv
+    edge = ny * nl * HW
+    total = ny * nl * nx
+    low = total + place * HW + x + HW
+    high = total + edge + place * HW + x - nx
+    code = jnp.where(x < 0, low, jnp.where(x >= nx, high, place * nx + x))
+    return jnp.where(inside, code, -1).T
+
+
+def inner_kernel(dims, wide, col_ref, row_ref, lev_ref, foot_ref, rows_ref, out_ref, same_ref, codes):
     step = pl.program_id(0)
 
     @pl.when(step == 0)
     def _():
+        code = codes_of(*dims, col_ref, row_ref, lev_ref, foot_ref)
         for k in range(codes.shape[0]):
-            codes[k] = jnp.broadcast_to(code_ref[:, k : k + 1], codes.shape[1:])
-        out_ref[...] = jnp.zeros_like(out_ref)
-
-    wide = rows_ref.shape[0]
+            codes[k] = jnp.broadcast_to(code[:, k : k + 1], codes.shape[1:])
+
     parts = [codes[k] for k in range(codes.shape[0])]
     select = jnp.concatenate([hits_of(parts, step * wide + c, 128) for c in range(0, wide, 128)], axis=1)
-    out_ref[...] += jnp.dot(select, rows_ref[...], preferred_element_type=F32)
-
-
-def inner(code, rows):
-    n_obs, slots = code.shape
+    rows = rows_ref[pl.ds(pl.multiple_of(step * wide, wide), wide), :]
+    part = jnp.dot(select, rows, preferred_element_type=F32)
+
+    @pl.when(step == 0)
+    def _():
+        out_ref[...] = part
+
+    @pl.when(step > 0)
+    def _():
+        out_ref[...] += part
+
+
+VM = pl.BlockSpec(memory_space=pltpu.VMEM)
+
+
+def inner(dims, index, rows):
+    slots, n_obs = index[3].shape
     total, members = rows.shape
-    wide = 256
+    wide = 512
     return pl.pallas_call(
-        inner_kernel,
+        functools.partial(inner_kernel, dims, wide),
         out_shape=(
             jax.ShapeDtypeStruct((n_obs, members), F32),
             jax.ShapeDtypeStruct(rows.shape, rows.dtype),
         ),
         grid=(total // wide,),
-        in_specs=[
-            pl.BlockSpec((n_obs, slots), lambda i: (0, 0)),
-            pl.BlockSpec((wide, members), lambda i: (i, 0)),
-        ],
-        out_specs=(
-            pl.BlockSpec((n_obs, members), lambda i: (0, 0)),
-            pl.BlockSpec(memory_space=pl.ANY),
-        ),
-        input_output_aliases={1: 1},
+        in_specs=[VM] * 5,
+        out_specs=(VM, pl.BlockSpec(memory_space=pl.ANY)),
+        input_output_aliases={4: 1},
         scratch_shapes=[pltpu.VMEM((slots, n_obs, 128), jnp.int32)],
+        compiler_params=pltpu.CompilerParams(vmem_limit_bytes=24 << 20),
         cost_estimate=pl.CostEstimate(flops=2 * 10**9, bytes_accessed=2 << 20, transcendentals=0),
-    )(code, rows)
-
-
-def edge_kernel(first, code_ref, before_ref, after_ref, inner_ref, out_ref):
-    n_obs, slots = code_ref.shape
-    members = inner_ref.shape[1]
+    )(*index, rows)
+
+
+def edge_kernel(dims, col_ref, row_ref, lev_ref, foot_ref, before_ref, after_ref, inner_ref, out_ref):
+    n_obs, members = inner_ref.shape
     wide = before_ref.shape[0]
-    codes = [jnp.broadcast_to(code_ref[:, k : k + 1], (n_obs, wide)) for k in range(slots)]
-    total = inner_ref[...]
-    total += jnp.dot(hits_of(codes, first, wide), before_ref[...], preferred_element_type=F32)
-    total += jnp.dot(hits_of(codes, first + wide, wide), after_ref[...], preferred_element_type=F32)
+    first = dims[1] * dims[2] * dims[3]
+    code = codes_of(*dims, col_ref, row_ref, lev_ref, foot_ref)
+    codes = [jnp.broadcast_to(code[:, k : k + 1], (n_obs, wide)) for k in range(code.shape[1])]
+    select = jnp.concatenate([hits_of(codes, first, wide), hits_of(codes, first + wide, wide)], axis=1)
+    rows = jnp.concatenate([before_ref[...], after_ref[...]], axis=0)
+    total = inner_ref[...] + jnp.dot(select, rows, preferred_element_type=F32)
     total = total * (1.0 / KF)
     mean = jnp.sum(total, axis=1, keepdims=True) * (1.0 / members)
     out_ref[:, :members] = (total - mean).astype(BF)
@@ -221,38 +250,30 @@
     out_ref[:, members:] = cols.astype(BF)
 
 
-def with_edges(first, code, before, after, part):
+def with_edges(dims, index, before, after, part):
     n_obs, members = part.shape
     return pl.pallas_call(
-        functools.partial(edge_kernel, first),
+        functools.partial(edge_kernel, dims),
         out_shape=jax.ShapeDtypeStruct((n_obs, members + 128), BF),
-        in_specs=[pl.BlockSpec(memory_space=pltpu.VMEM)] * 4,
-        out_specs=pl.BlockSpec(memory_space=pltpu.VMEM),
+        in_specs=[VM] * 7,
+        out_specs=VM,
+        compiler_params=pltpu.CompilerParams(vmem_limit_bytes=24 << 20),
         cost_estimate=pl.CostEstimate(flops=10**9, bytes_accessed=1 << 20, transcendentals=0),
-    )(code, before, after, part)
+    )(*index, before, after, part)
 
 
 def observe(grid, obs_col, obs_row, foot_off, obs_lev, ny_total):
     ny, nl, nx, members = grid.shape
-    span = 2 * DY + 1
-    x = obs_col[:, None] + foot_off // span - HW
-    y = jnp.clip(obs_row[:, None] + foot_off % span - DY, 0, ny_total - 1) - lax.axis_index("gy") * ny
-    lv = obs_lev[:, None] - lax.axis_index("lev") * nl
-    inside = (y >= 0) & (y < ny) & (lv >= 0) & (lv < nl)
-    place = y * nl + lv
-    edge = ny * nl * HW
-    total = ny * nl * nx
-    low = total + place * HW + x + HW
-    high = total + edge + place * HW + x - nx
-    code = jnp.where(x < 0, low, jnp.where(x >= nx, high, place * nx + x))
-    code = jnp.where(inside, code, -1)
+    dims = (ny_total, ny, nl, nx)
+    index = (obs_col[None, :], obs_row[None, :], obs_lev[None, :], foot_off.T)
     size = lax.axis_size("gx")
     up = [(i, (i + 1) % size) for i in range(size)]
     down = [(j, i) for i, j in up]
+    edge = ny * nl * HW
     before = lax.ppermute(grid[:, :, nx - HW :], "gx", up).reshape(edge, members)
     after = lax.ppermute(grid[:, :, :HW], "gx", down).reshape(edge, members)
-    part, rows = inner(code, grid.reshape(total, members))
-    return with_edges(total, code, before, after, part), rows
+    part, rows = inner(dims, index, grid.reshape(ny * nl * nx, members))
+    return with_edges(dims, index, before, after, part), rows
 
 
 def share(msg):
@@ -261,65 +282,80 @@
         size = lax.axis_size(axis)
         got = swap(msg.reshape(size, msg.shape[0] // size, msg.shape[1]), axis)
         msg = pack(*unpack_sum(got, members))
-    size = lax.axis_size("gy")
-    msg = swap(jnp.broadcast_to(msg[None], (size,) + msg.shape), "gy").reshape(-1, msg.shape[1])
-    msg = lax.all_gather(msg, "lev", axis=0, tiled=True)
+    for axis in ("gy", "lev"):
+        size = lax.axis_size(axis)
+        msg = swap(jnp.broadcast_to(msg[None], (size,) + msg.shape), axis).reshape(-1, msg.shape[1])
     return msg[:, :members], jnp.sum(msg[:, members : members + 3].astype(F32), axis=1)
 
 
 def update_kernel(got_ref, loc_ref, y_ref, z_ref, w_ref, out_ref, mean_ref):
-    nx = got_ref.shape[3]
-    members = got_ref.shape[4]
-    nl = got_ref.shape[2]
-    levels = got_ref.shape[0] * nl
-    rows = nx * levels
+    parts, ny, nl, nx, members = got_ref.shape
+    levels = parts * nl
+    part = 16
+    rows = part * levels
+    step = pl.program_id(0)
     ii = lax.broadcasted_iota(jnp.int32, (rows, rows), 0)
     jj = lax.broadcasted_iota(jnp.int32, (rows, rows), 1)
-    order = jnp.where(jj == (ii % levels) * nx + ii // levels, 1.0, 0.0).astype(BF)
-    for y in range(got_ref.shape[1]):
-        block = jnp.concatenate([got_ref[lv // nl, y, lv % nl] for lv in range(levels)], axis=0)
-        block = jnp.dot(order, block, preferred_element_type=F32)
-        xbar = jnp.sum(block, axis=1, keepdims=True) * (1.0 / members)
-        anom = (block - xbar).astype(BF)
-        cross = mm(anom, y_ref[...], NT, None) * (1.0 / (members - 1))
+    order = jnp.where(jj == (ii % levels) * part + ii // levels, 1.0, 0.0).astype(BF)
+    blocks, weights = [], []
+    for y in range(ny):
+        for x in range(0, nx, part):
+            block = jnp.concatenate(
+                [got_ref[lv // nl, y, lv % nl, x : x + part] for lv in range(levels)], axis=0
+            )
+            blocks.append(jnp.dot(order, block, preferred_element_type=F32))
         weight = loc_ref[y].astype(F32)
-        weight = jnp.broadcast_to(weight[:, None, :], (nx, levels, weight.shape[1])).reshape(rows, weight.shape[1])
-        gain = (cross * weight).astype(BF)
-        result = anom.astype(F32) - jnp.dot(gain, z_ref[...], preferred_element_type=F32)
-        out_ref[:, y] = result.reshape(nx, levels, members).astype(BF)
-        shift = jnp.sum(mm(gain, w_ref[...], NT, None), axis=1, keepdims=True)
-        mean = jnp.where(ii == jj, xbar + shift, 0.0)
-        mean_ref[0, y : y + 1] = jnp.sum(mean, axis=0, keepdims=True)
+        weight = jnp.broadcast_to(weight[:, None, :], (nx, levels, weight.shape[1]))
+        weights.append(weight.reshape(nx * levels, weight.shape[2]))
+    block = jnp.concatenate(blocks, axis=0)
+    xbar = jnp.sum(block, axis=1, keepdims=True) * (1.0 / members)
+    anom = (block - xbar).astype(BF)
+    cross = mm(anom, y_ref[...], NT, None) * (1.0 / (members - 1))
+    gain = (cross * jnp.concatenate(weights, axis=0)).astype(BF)
+    result = anom.astype(F32) - jnp.dot(gain, z_ref[...], preferred_element_type=F32)
+    result = result.reshape(ny, nx, levels, members).astype(BF)
+    column = xbar + jnp.sum(mm(gain, w_ref[...], NT, None), axis=1, keepdims=True)
+    count = nx * levels
+    lane = lax.broadcasted_iota(jnp.int32, (count, 128), 1)
+    place = lax.broadcasted_iota(jnp.int32, (count, 128), 0) // levels + step * nx
+
+    @pl.when(step == 0)
+    def _():
+        mean_ref[...] = jnp.zeros_like(mean_ref)
+
+    for y in range(ny):
+        out_ref[:, y] = result[y]
+        spread = jnp.where(lane == place, column[y * count : (y + 1) * count], 0.0)
+        mean_ref[y] += jnp.sum(spread.reshape(nx, levels, 128), axis=0)
 
 
 def update(got, loc, ybf, zmat, wrows):
     parts, ny, nl, nx, members = got.shape
     n_obs = ybf.shape[0]
     levels = parts * nl
-    wide = 16
-    whole = lambda i: (0, 0)
+    wide = 32
     out, mean = pl.pallas_call(
         update_kernel,
         out_shape=(
             jax.ShapeDtypeStruct((nx, ny, levels, members), BF),
-            jax.ShapeDtypeStruct((nx // wide, ny, wide * levels), F32),
+            jax.ShapeDtypeStruct((ny, levels, nx), F32),
         ),
         grid=(nx // wide,),
         in_specs=[
             pl.BlockSpec((parts, ny, nl, wide, members), lambda i: (0, 0, 0, i, 0)),
             pl.BlockSpec((ny, wide, n_obs), lambda i: (0, i, 0)),
-            pl.BlockSpec(ybf.shape, whole),
-            pl.BlockSpec(zmat.shape, whole),
-            pl.BlockSpec(wrows.shape, whole),
+            VM,
+            VM,
+            VM,
         ],
         out_specs=(
             pl.BlockSpec((wide, ny, levels, members), lambda i: (i, 0, 0, 0)),
-            pl.BlockSpec((1, ny, wide * levels), lambda i: (i, 0, 0)),
+            pl.BlockSpec((ny, levels, nx), lambda i: (0, 0, 0)),
         ),
+        compiler_params=pltpu.CompilerParams(vmem_limit_bytes=24 << 20),
         cost_estimate=pl.CostEstimate(flops=3 * 10**9, bytes_accessed=5 << 20, transcendentals=0),
     )(got, loc, ybf, zmat, wrows)
-    mean = mean.reshape(nx // wide, ny, wide, levels).transpose(0, 2, 1, 3).reshape(nx, ny, levels)
-    return mean, out
+    return mean.transpose(2, 0, 1), out
 
 
 def local(state, obs_col, obs_row, foot_off, obs_lev, obs_val, obs_err, loc):

time: 153 us -> 131 us (0.86)
  Pallas kernels: 51.9 us -> 40.2 us
  local copies, waits for them, and re-layouts: 13.2 us -> 7.8 us
  blocking collectives: 76 us -> 73.8 us
  other arithmetic: 2.72 us -> 0.57 us
    all_gather x1 -> x0, blocking collectives: 13.3 us -> none  [share(): msg = lax.all_gather(msg, 'lev', axis=0, tiled=True)]
    all_to_all x3 -> x4, blocking collectives: 62.7 us -> 73.8 us  [swap(): return lax.all_to_all(array, axis, split_axis=0, concat_axis=0, tiled=True)]
    pallas_call x1, Pallas kernels: 13.1 us -> 6.35 us  [update(): pl.pallas_call(update_kernel, out_shape=(jax.ShapeDtypeStruct((nx, ny, le...]
    pallas_call x2, Pallas kernels: 11.9 us -> 7.75 us  [the longest x1 6.5 us: inner(): pl.pallas_call(functools.partial(inner_kernel, dims, wide), out_shape=(ja...]
    unnamed x24 -> x20, local copies, waits for them, and re-layouts: 5.15 us -> 2.04 us
  transfers between devices with their start and end apart: 3 -> 3, of which waited for: 0 -> 0; matrix products, arithmetic and copies ran while one was open for 6% -> 3% of each run, Pallas kernels for 23% -> 25%
where the time goes in v1:
time: 131 us; the launch traced here: 130 us
  blocking collectives  73.8 us (56%)
  Pallas kernels  40.2 us (31%)
  local copies, waits for them, and re-layouts  7.8 us (6%)
  starting transfers between devices  6.9 us (5%)
    all_to_all x4, blocking collectives, swap(): return lax.all_to_all(array, axis, split_axis=0, concat_axis=0, tiled=True)  73.8 us
    pallas_call x1, Pallas kernels, solve(): pl.pallas_call(solve_kernel, out_shape=(jax.ShapeDtypeStruct((n, M), BF),...  26.1 us
    pallas_call x1, Pallas kernels, inner(): pl.pallas_call(functools.partial(inner_kernel, dims, wide), out_shape=(ja...  6.5 us
    pallas_call x1, Pallas kernels, update(): pl.pallas_call(update_kernel, out_shape=(jax.ShapeDtypeStruct((nx, ny, le...  6.35 us
    all_to_all x1, starting transfers between devices, swap(): return lax.all_to_all(array, axis, split_axis=0, concat_axis=0, tiled=True)  5.18 us
    optimization_barrier x1, local copies, waits for them, and re-layouts, local(): grid = lax.optimization_barrier(jnp.transpose(state, (1, 2, 0, 3)))  4.07 us
  transfers between devices with their start and end apart: 3, of which 0 were waited for; matrix products, arithmetic and copies ran while one was open for 3% of the time, Pallas kernels for 25%

profile of v1, /device:TPU:10, one launch (start us, length us, event | category | flops | bytes accessed | tf_op | source)
XLA Modules:
  0.0 130.2 jit_solution(14497784470144884687)
XLA Ops:
  0.6 1.2 fusion.8
  1.9 1.7 %collective-permute-start.1 = (bf16[8,2,8,512]{3,1,0,2:T(2,128)(2,1)S(1)}, bf16[8,2,8,512]{3,1,0,2:T(2,128)(2,1)S(1)}, u32[]{:S(2)}, u32[]{:S(2)}) collective-permute-start(bf16[8,2,8,512]{3,1,0,2:T(2,128)(2,1)S(1)} %get-tuple-element.20), channel_id=1, source_target_pairs={{64,0},{128,64},{192,128},{256,192},{320,256},{384,320},{448,384},... | collective-permute-start | bytes 393224 | tf_op jit(solution)/shard_map/ppermute | solution.py:274
  3.6 4.1 %copy.24 = bf16[8,2,128,512]{3,2,1,0:T(8,128)(2,1)} copy(bf16[8,2,128,512]{3,1,0,2:T(2,128)(2,1)} %bitcast.47) | data formatting | bytes 4194304 | tf_op jit(solution)/shard_map/optimization_barrier | solution.py:363
  7.7 6.5 %shard_map.95 = (f32[512,512]{1,0:T(8,128)S(1)}, bf16[2048,512]{1,0:T(8,128)(2,1)}) custom-call(s32[1,512]{1,0:T(1,128)S(1)} %bitcast.40, s32[1,512]{1,0:T(1,128)S(1)} %bitcast.42, s32[1,512]{1,0:T(1,128)S(1)} %bitcast.44, s32[8,512]{1,0:T(8,128)S(1)} %bitcast.38, bf16[2048,512]{1,0:T(8,128)(2,1)} %bitcast.5.rows_ref), custom_call_target="tpu_custom_call", output_to_operand_aliasing={{1}: (4, {})} | custom-call | flops 2000000000 | bytes 2097152 | tf_op jit(solution)/shard_map/pallas_call | solution.py:218
  14.2 0.1 copy.25
  14.3 0.1 copy.26
  14.4 1.3 shard_map.96
  15.6 14.2 %all_to_all.25 = bf16[4,128,640]{2,1,0:T(8,128)(2,1)S(1)} all-to-all(bf16[4,128,640]{2,1,0:T(8,128)(2,1)S(1)} %bitcast.31), channel_id=1, replica_groups=mesh['gx'=8,'gy'=16,'lev'=4] {'lev'}, dimensions={0} | all-to-all | bytes 1310720 | tf_op jit(solution)/shard_map/all_to_all | solution.py:160
  29.8 0.1 convert_reduce_fusion
  29.9 0.1 slice_reduce_fusion
  30.1 0.1 copy.32
  30.2 29.7 %all_to_all.26 = bf16[16,8,640]{2,1,0:T(8,128)(2,1)S(1)} all-to-all(bf16[16,8,640]{2,1,0:T(8,128)(2,1)S(1)} %pad_maximum_fusion), channel_id=1, replica_groups=mesh['gx'=8,'gy'=16,'lev'=4] {'gy'}, dimensions={0} | all-to-all | bytes 327680 | tf_op jit(solution)/shard_map/all_to_all | solution.py:160
  60.0 0.1 slice_reduce_fusion.1
  60.1 0.1 copy.28
  60.2 0.1 fusion.6
  60.3 18.7 %all_to_all.27 = bf16[16,8,640]{2,1,0:T(8,128)(2,1)S(1)} all-to-all(bf16[16,8,640]{2,1,0:T(8,128)(2,1)S(1)} %broadcast_in_dim.34), channel_id=1, replica_groups=mesh['gx'=8,'gy'=16,'lev'=4] {'gy'}, dimensions={0} | all-to-all | bytes 327680 | tf_op jit(solution)/shard_map/all_to_all | solution.py:160
  79.1 11.2 %all_to_all.28 = bf16[4,128,640]{2,1,0:T(8,128)(2,1)S(1)} all-to-all(bf16[4,128,640]{2,1,0:T(8,128)(2,1)S(1)} %broadcast_in_dim.36), channel_id=1, replica_groups=mesh['gx'=8,'gy'=16,'lev'=4] {'lev'}, dimensions={0} | all-to-all | bytes 1310720 | tf_op jit(solution)/shard_map/all_to_all | solution.py:160
  90.3 0.1 convert_reduce_fusion.2
  90.4 5.2 %all-to-all-start.4 = ((bf16[4,2,2,128,512]{4,3,2,1,0:T(8,128)(2,1)}), bf16[4,2,2,128,512]{4,3,2,1,0:T(8,128)(2,1)S(1)}, u32[]{:S(2)}, u32[]{:S(2)}) async-start(bf16[4,2,2,128,512]{4,3,2,1,0:T(8,128)(2,1)} %bitcast.15), calls=%async_computation.4 | async-start | bytes 4194304 | tf_op jit(solution)/shard_map/all_to_all | solution.py:160
  95.6 0.1 copy.31.errc_ref
  95.8 26.1 %shard_map.97 = (bf16[512,512]{1,0:T(8,128)(2,1)S(1)}, bf16[16,512]{1,0:T(8,128)(2,1)S(1)}) custom-call(bf16[512,512]{1,0:T(8,128)(2,1)S(1)} %slice.40.y_ref, f32[1,512]{1,0:T(1,128)S(1)} %bitcast.37, f32[1,512]{1,0:T(1,128)S(1)} %bitcast.36, f32[512,1]{1,0:T(8,128)S(1)} %copy.31.errc_ref), custom_call_target="tpu_custom_call" | custom-call | flops 6000000000 | bytes 2097152 | tf_op jit(solution)/shard_map/pallas_call | solution.py:132
  122.0 0.8 copy-done.5
  122.8 1.0 copy-done.6
  123.8 6.4 %shard_map.98 = (bf16[128,2,8,512]{3,2,1,0:T(8,128)(2,1)}, f32[2,8,128]{2,1,0:T(8,128)}) custom-call(bf16[4,2,2,128,512]{4,3,2,1,0:T(8,128)(2,1)S(1)} %all-to-all-done.4.got_ref, bf16[2,128,512]{2,1,0:T(8,128)(2,1)S(1)} %bitcast.32, bf16[512,512]{1,0:T(8,128)(2,1)S(1)} %slice.40.y_ref, bf16[512,512]{1,0:T(8,128)(2,1)S(1)} %copy-done.6, ...), custom_call_target="tpu_custom_call" | custom-call | flops 3000000000 | bytes 5242880 | tf_op jit(solution)/shard_map/pallas_call | solution.py:337
  (34 shorter events, 0.3 us)
Async XLA Ops:
  1.8 12.4 %collective-permute-start = (bf16[8,2,8,512]{3,1,0,2:T(2,128)(2,1)S(1)}, bf16[8,2,8,512]{3,1,0,2:T(2,128)(2,1)S(1)}, u32[]{:S(2)}, u32[]{:S(2)}) collective-permute-start(bf16[8,2,8,512]{3,1,0,2:T(2,128)(2,1)S(1)} %get-tuple-element.21), channel_id=1, source_target_pairs={{0,64},{64,128},{128,192},{192,256},{256,320},{320,384},{384,448},... | collective-permute-start | bytes 393224 | tf_op jit(solution)/shard_map/ppermute | solution.py:273
  1.8 5.8 %copy-start.1 = (s32[512,8]{0,1:T(8,128)S(1)}, s32[512,8]{0,1:T(8,128)}, u32[]{:S(2)}) copy-start(s32[512,8]{0,1:T(8,128)} %param.11) | copy-start | bytes 49156
  1.8 5.8 %copy-start.2 = (s32[512]{0:T(512)S(1)}, s32[512]{0:T(512)}, u32[]{:S(2)}) copy-start(s32[512]{0:T(512)} %param.9) | copy-start | bytes 6148
  1.9 5.8 %copy-start.3 = (s32[512]{0:T(512)S(1)}, s32[512]{0:T(512)}, u32[]{:S(2)}) copy-start(s32[512]{0:T(512)} %param.10) | copy-start | bytes 6148
  1.9 5.8 %copy-start.4 = (s32[512]{0:T(512)S(1)}, s32[512]{0:T(512)}, u32[]{:S(2)}) copy-start(s32[512]{0:T(512)} %param.12) | copy-start | bytes 6148
  1.9 12.4 %collective-permute-start.1 = (bf16[8,2,8,512]{3,1,0,2:T(2,128)(2,1)S(1)}, bf16[8,2,8,512]{3,1,0,2:T(2,128)(2,1)S(1)}, u32[]{:S(2)}, u32[]{:S(2)}) collective-permute-start(bf16[8,2,8,512]{3,1,0,2:T(2,128)(2,1)S(1)} %get-tuple-element.20), channel_id=1, source_target_pairs={{64,0},{128,64},{192,128},{256,192},{320,256},{384,320},{448,384},... | collective-permute-start | bytes 393224 | tf_op jit(solution)/shard_map/ppermute | solution.py:274
  90.4 5.2 %copy-start = (f32[512]{0:T(512)S(1)}, f32[512]{0:T(512)}, u32[]{:S(2)}) copy-start(f32[512]{0:T(512)} %param.14) | copy-start | bytes 6148
  90.4 5.4 %copy-start.7 = (bf16[128,2,512]{2,1,0:T(2,128)(2,1)S(1)}, bf16[128,2,512]{2,1,0:T(2,128)(2,1)}, u32[]{:S(2)}) copy-start(bf16[128,2,512]{2,1,0:T(2,128)(2,1)} %param.15) | copy-start | bytes 786436
  90.4 5.4 %copy-start.8 = (f32[512]{0:T(512)S(1)}, f32[512]{0:T(512)}, u32[]{:S(2)}) copy-start(f32[512]{0:T(512)} %param.13) | copy-start | bytes 6148
  90.4 32.3 %all-to-all-start.4 = ((bf16[4,2,2,128,512]{4,3,2,1,0:T(8,128)(2,1)}), bf16[4,2,2,128,512]{4,3,2,1,0:T(8,128)(2,1)S(1)}, u32[]{:S(2)}, u32[]{:S(2)}) async-start(bf16[4,2,2,128,512]{4,3,2,1,0:T(8,128)(2,1)} %bitcast.15), calls=%async_computation.4 | async-start | bytes 4194304 | tf_op jit(solution)/shard_map/all_to_all | solution.py:160
  122.0 0.8 copy-start.5
  122.8 1.0 copy-start.6

commit v2 on v1

--- a/solution.py
+++ b/solution.py
@@ -60,19 +60,58 @@
     X=[X[v]*rs[v] for v in range(nv)]
     return jnp.concatenate(X,0)[:,:SUB], jnp.concatenate(G,0)[:,:SUB]
 
-def solve_kernel(y_ref, innov_ref, errr_ref, errc_ref, z_ref, w_ref, A, U, Li, Gi):
+def mm_split(a,b,dims):
+    ah,al=halves(a)
+    bh,bl=halves(b)
+    return mm(ah,bh,dims,None)+(mm(ah,bl,dims,None)+mm(al,bh,dims,None))
+
+def solve_kernel(y_ref, innov_ref, errr_ref, errc_ref, z_ref, w_ref, A, U, Li, Gi, S, V):
     n=A.shape[0]
     M=y_ref.shape[1]
     y=y_ref[...]
     A[...]=mm(y,y,NT,None)*(1.0/(M-1))
-    Li[...]=jnp.zeros_like(Li)
-    Gi[...]=jnp.zeros_like(Gi)
     sup=n//SUP
     ii=lax.broadcasted_iota(jnp.int32,(SUP,SUP),0)
     jj=lax.broadcasted_iota(jnp.int32,(SUP,SUP),1)
     for s in range(sup):
         w0=s*SUP
         A[w0:w0+SUP,w0:w0+SUP]=A[w0:w0+SUP,w0:w0+SUP]+jnp.where(ii==jj,errr_ref[:,w0:w0+SUP],0.0)
+    Li[...]=jnp.zeros_like(Li)
+    Gi[...]=jnp.zeros_like(Gi)
+
+    def lower(w0,q):
+        def run():
+            r=slice(q,q+SUP)
+            A[r,q:n]=A[r,q:n]-mm(U[w0:w0+SUP,r],U[w0:w0+SUP,q:n],TN)
+        return run
+
+    def widen(B,w0,size):
+        def run():
+            L=U[w0:w0+SUP,w0:w0+SUP].T
+            T=B[w0:w0+SUP,:]
+            mask=((ii//(2*size))==(jj//(2*size)))&((ii//size)>(jj//size))
+            B[w0:w0+SUP,:]=T-mm(T,mm(jnp.where(mask,L,0.0),T,NN),NN)
+        return run
+
+    def ahead_s(w0):
+        def run():
+            r=slice(w0,w0+SUP)
+            rest=y_ref[r,:].astype(F32)
+            if w0:
+                rest=rest-mm_split(U[:w0,r],S[:w0,:],TN)
+            S[r,:]=mm_split(Gi[r,:],rest,NN)
+        return run
+
+    def ahead_v(w0):
+        def run():
+            r=slice(w0,w0+SUP)
+            rest=jnp.broadcast_to(innov_ref[r,:],(SUP,128))
+            if w0:
+                rest=rest-mm(U[:w0,r],V[:w0,:],TN)
+            V[r,:]=mm(Li[r,:],rest,NN)
+        return run
+
+    waiting=[]
     for s in range(sup):
         w0=s*SUP
         for t in range(SUP//SUB):
@@ -80,52 +119,41 @@
             R=A[k0:k0+SUB,w0:n]
             if t:
                 R=R-mm(U[w0:k0,k0:k0+SUB],U[w0:k0,w0:n],TN)
+            for task in waiting[:2]:
+                task()
+            waiting=waiting[2:]
             sq=jnp.broadcast_to(jnp.sqrt(errc_ref[k0:k0+SUB,:]),(SUB,128))
             sq=[sq[8*v:8*v+8] for v in range(SUB//8)]
             x,g=factor_block(R,t*SUB,sq)
             U[k0:k0+SUB,w0:n]=mm(x,R,NN)
-            Li[k0:k0+SUB,k0:k0+SUB]=x
-            Gi[k0:k0+SUB,k0:k0+SUB]=g
+            Li[k0:k0+SUB,t*SUB:(t+1)*SUB]=x
+            Gi[k0:k0+SUB,t*SUB:(t+1)*SUB]=g
         w1=w0+SUP
         if w1<n:
-            A[w1:n,w1:n]=A[w1:n,w1:n]-mm(U[w0:w1,w1:n],U[w0:w1,w1:n],TN)
-    for s in range(sup):
-        w0=s*SUP
-        L=U[w0:w0+SUP,w0:w0+SUP].T
-        for B in (Li,Gi):
-            T=B[w0:w0+SUP,w0:w0+SUP]
-            size=SUB
-            while size<SUP:
-                mask=((ii//(2*size))==(jj//(2*size)))&((ii//size)>(jj//size))
-                N=jnp.where(mask,L,0.0)
-                T=T-mm(T,mm(N,T,NN),NN)
-                size*=2
-            B[w0:w0+SUP,w0:w0+SUP]=T
-    size=SUP
-    while size<n:
-        for a0 in range(0,n,2*size):
-            b0=a0+size; b1=b0+size
-            for B in (Li,Gi):
-                t=mm(U[a0:b0,b0:b1],B[a0:b0,a0:b0],TN)
-                B[b0:b1,a0:b0]=-mm(B[b0:b1,b0:b1],t,NN)
-        size*=2
-    gh,gl=halves(Gi[...])
-    S=[]
-    for s in range(sup):
-        r,k=slice(s*SUP,(s+1)*SUP),(s+1)*SUP
-        S.append(mm(gh[r,:k],y[:k],NN,None)+mm(gl[r,:k],y[:k],NN,None))
-    sh,sl=halves(jnp.concatenate(S,0))
-    lh,ll=halves(Li[...].T)
-    v=jnp.sum(Li[...]*innov_ref[...],axis=1,keepdims=True)
-    w=jnp.sum(Li[...]*v,axis=0,keepdims=True)
+            lower(w0,w1)()
+        for task in waiting:
+            task()
+        waiting=[lower(w0,q) for q in range(w1+SUP,n,SUP)]
+        waiting+=[widen(Gi,w0,SUB),widen(Li,w0,SUB),widen(Gi,w0,2*SUB),widen(Li,w0,2*SUB),ahead_s(w0),ahead_v(w0)]
+    for task in waiting:
+        task()
+    for s in reversed(range(sup)):
+        r=slice(s*SUP,(s+1)*SUP)
+        k=(s+1)*SUP
+        lt=Li[r,:].T
+        rest,tail=S[r,:],V[r,:]
+        if k<n:
+            rest=rest-mm_split(U[r,k:],S[k:,:],NN)
+            tail=tail-mm(U[r,k:],V[k:,:],NN)
+        z=mm_split(lt,rest,NN)
+        S[r,:]=z
+        z_ref[r,:]=z.astype(z_ref.dtype)
+        V[r,:]=mm(lt,tail,NN)
+    w=V[...].T[0:1,:]
     hi=w.astype(BF).astype(F32)
     mid=(w-hi).astype(BF).astype(F32)
     pick=lax.broadcasted_iota(jnp.int32,w_ref.shape,0)
     w_ref[...]=jnp.where(pick==0,hi,jnp.where(pick==1,mid,jnp.where(pick==2,w-hi-mid,0.0))).astype(BF)
-    for s in range(sup):
-        r,k=slice(s*SUP,(s+1)*SUP),s*SUP
-        z=mm(lh[r,k:],sh[k:],NN,None)+(mm(lh[r,k:],sl[k:],NN,None)+mm(ll[r,k:],sh[k:],NN,None))
-        z_ref[r,:]=z.astype(z_ref.dtype)
 
 def solve(y, innov, err):
     n,M=y.shape
@@ -133,10 +161,10 @@
         out_shape=(jax.ShapeDtypeStruct((n,M),BF),jax.ShapeDtypeStruct((16,n),BF)),
         in_specs=[pl.BlockSpec(memory_space=pltpu.VMEM)]*4,
         out_specs=(pl.BlockSpec(memory_space=pltpu.VMEM),)*2,
-        scratch_shapes=[pltpu.VMEM((n,n),F32)]*4,
+        scratch_shapes=[pltpu.VMEM((n,n),F32)]*2+[pltpu.VMEM((n,SUP),F32)]*2+[pltpu.VMEM((n,M),F32),pltpu.VMEM((n,128),F32)],
         compiler_params=pltpu.CompilerParams(vmem_limit_bytes=24<<20),
         cost_estimate=pl.CostEstimate(flops=6*10**9,bytes_accessed=2<<20,transcendentals=0),
-    )(y, innov[None,:], err[None,:], err[:,None])
+    )(y, innov[:,None], err[None,:], err[:,None])
 
 
 def split3(x):

time: 131 us -> 128 us (0.977)
  Pallas kernels: 40.2 us -> 37 us
    pallas_call x1, Pallas kernels: 26.1 us -> 22.9 us  [solve(): pl.pallas_call(solve_kernel, out_shape=(jax.ShapeDtypeStruct((n, M), BF),...]
  transfers between devices with their start and end apart: 3 -> 3, of which waited for: 0 -> 0; matrix products, arithmetic and copies ran while one was open for 3% -> 4% of each run, Pallas kernels for 25% -> 23%
where the time goes in v2:
time: 128 us; the launch traced here: 127 us
  blocking collectives  73.8 us (58%)
  Pallas kernels  37 us (29%)
  local copies, waits for them, and re-layouts  7.96 us (6%)
  starting transfers between devices  6.9 us (5%)
    all_to_all x4, blocking collectives, swap(): return lax.all_to_all(array, axis, split_axis=0, concat_axis=0, tiled=True)  73.8 us
    pallas_call x1, Pallas kernels, solve(): pl.pallas_call(solve_kernel, out_shape=(jax.ShapeDtypeStruct((n, M), BF),...  22.9 us
    pallas_call x1, Pallas kernels, inner(): pl.pallas_call(functools.partial(inner_kernel, dims, wide), out_shape=(ja...  6.5 us
    pallas_call x1, Pallas kernels, update(): pl.pallas_call(update_kernel, out_shape=(jax.ShapeDtypeStruct((nx, ny, le...  6.35 us
    all_to_all x1, starting transfers between devices, swap(): return lax.all_to_all(array, axis, split_axis=0, concat_axis=0, tiled=True)  5.18 us
    optimization_barrier x1, local copies, waits for them, and re-layouts, local(): grid = lax.optimization_barrier(jnp.transpose(state, (1, 2, 0, 3)))  4.07 us
  transfers between devices with their start and end apart: 3, of which 0 were waited for; matrix products, arithmetic and copies ran while one was open for 4% of the time, Pallas kernels for 23%

profile of v2, /device:TPU:10, one launch (start us, length us, event | category | flops | bytes accessed | tf_op | source)
XLA Modules:
  0.0 127.1 jit_solution(17500605441169742340)
XLA Ops:
  0.6 1.2 fusion.8
  1.9 1.7 %collective-permute-start.1 = (bf16[8,2,8,512]{3,1,0,2:T(2,128)(2,1)S(1)}, bf16[8,2,8,512]{3,1,0,2:T(2,128)(2,1)S(1)}, u32[]{:S(2)}, u32[]{:S(2)}) collective-permute-start(bf16[8,2,8,512]{3,1,0,2:T(2,128)(2,1)S(1)} %get-tuple-element.20), channel_id=1, source_target_pairs={{64,0},{128,64},{192,128},{256,192},{320,256},{384,320},{448,384},... | collective-permute-start | bytes 393224 | tf_op jit(solution)/shard_map/ppermute | solution.py:302
  3.6 4.1 %copy.25 = bf16[8,2,128,512]{3,2,1,0:T(8,128)(2,1)} copy(bf16[8,2,128,512]{3,1,0,2:T(2,128)(2,1)} %bitcast.46) | data formatting | bytes 4194304 | tf_op jit(solution)/shard_map/optimization_barrier | solution.py:391
  7.7 6.5 %shard_map.95 = (f32[512,512]{1,0:T(8,128)S(1)}, bf16[2048,512]{1,0:T(8,128)(2,1)}) custom-call(s32[1,512]{1,0:T(1,128)S(1)} %bitcast.39, s32[1,512]{1,0:T(1,128)S(1)} %bitcast.41, s32[1,512]{1,0:T(1,128)S(1)} %bitcast.43, s32[8,512]{1,0:T(8,128)S(1)} %bitcast.37, bf16[2048,512]{1,0:T(8,128)(2,1)} %bitcast.5.rows_ref), custom_call_target="tpu_custom_call", output_to_operand_aliasing={{1}: (4, {})} | custom-call | flops 2000000000 | bytes 2097152 | tf_op jit(solution)/shard_map/pallas_call | solution.py:246
  14.2 0.1 copy.26
  14.3 0.1 copy.27
  14.4 1.3 shard_map.96
  15.6 14.2 %all_to_all.25 = bf16[4,128,640]{2,1,0:T(8,128)(2,1)S(1)} all-to-all(bf16[4,128,640]{2,1,0:T(8,128)(2,1)S(1)} %bitcast.31), channel_id=1, replica_groups=mesh['gx'=8,'gy'=16,'lev'=4] {'lev'}, dimensions={0} | all-to-all | bytes 1310720 | tf_op jit(solution)/shard_map/all_to_all | solution.py:188
  29.9 0.1 slice_reduce_fusion
  30.1 0.1 copy.34
  30.2 29.7 %all_to_all.26 = bf16[16,8,640]{2,1,0:T(8,128)(2,1)S(1)} all-to-all(bf16[16,8,640]{2,1,0:T(8,128)(2,1)S(1)} %pad_maximum_fusion), channel_id=1, replica_groups=mesh['gx'=8,'gy'=16,'lev'=4] {'gy'}, dimensions={0} | all-to-all | bytes 327680 | tf_op jit(solution)/shard_map/all_to_all | solution.py:188
  60.0 0.1 slice_reduce_fusion.1
  60.1 0.1 copy.29
  60.2 0.1 fusion.6
  60.3 18.7 %all_to_all.27 = bf16[16,8,640]{2,1,0:T(8,128)(2,1)S(1)} all-to-all(bf16[16,8,640]{2,1,0:T(8,128)(2,1)S(1)} %broadcast_in_dim.34), channel_id=1, replica_groups=mesh['gx'=8,'gy'=16,'lev'=4] {'gy'}, dimensions={0} | all-to-all | bytes 327680 | tf_op jit(solution)/shard_map/all_to_all | solution.py:188
  79.1 11.2 %all_to_all.28 = bf16[4,128,640]{2,1,0:T(8,128)(2,1)S(1)} all-to-all(bf16[4,128,640]{2,1,0:T(8,128)(2,1)S(1)} %broadcast_in_dim.36), channel_id=1, replica_groups=mesh['gx'=8,'gy'=16,'lev'=4] {'lev'}, dimensions={0} | all-to-all | bytes 1310720 | tf_op jit(solution)/shard_map/all_to_all | solution.py:188
  90.3 0.1 convert_reduce_fusion.2
  90.4 5.2 %all-to-all-start.4 = ((bf16[4,2,2,128,512]{4,3,2,1,0:T(8,128)(2,1)}), bf16[4,2,2,128,512]{4,3,2,1,0:T(8,128)(2,1)S(1)}, u32[]{:S(2)}, u32[]{:S(2)}) async-start(bf16[4,2,2,128,512]{4,3,2,1,0:T(8,128)(2,1)} %bitcast.15), calls=%async_computation.4 | async-start | bytes 4194304 | tf_op jit(solution)/shard_map/all_to_all | solution.py:188
  95.6 0.1 copy.33.errc_ref
  95.8 0.1 copy.32.innov_ref
  96.0 22.9 %shard_map.97 = (bf16[512,512]{1,0:T(8,128)(2,1)S(1)}, bf16[16,512]{1,0:T(8,128)(2,1)S(1)}) custom-call(bf16[512,512]{1,0:T(8,128)(2,1)S(1)} %slice.40.y_ref, f32[512,1]{1,0:T(8,128)S(1)} %copy.32.innov_ref, f32[1,512]{1,0:T(1,128)S(1)} %bitcast.36, f32[512,1]{1,0:T(8,128)S(1)} %copy.33.errc_ref), custom_call_target="tpu_custom_call" | custom-call | flops 6000000000 | bytes 2097152 | tf_op jit(solution)/shard_map/pallas_call | solution.py:160
  118.9 0.8 copy-done.5
  119.7 1.0 copy-done.6
  120.8 6.4 %shard_map.98 = (bf16[128,2,8,512]{3,2,1,0:T(8,128)(2,1)}, f32[2,8,128]{2,1,0:T(8,128)}) custom-call(bf16[4,2,2,128,512]{4,3,2,1,0:T(8,128)(2,1)S(1)} %all-to-all-done.4.got_ref, bf16[2,128,512]{2,1,0:T(8,128)(2,1)S(1)} %bitcast.32, bf16[512,512]{1,0:T(8,128)(2,1)S(1)} %slice.40.y_ref, bf16[512,512]{1,0:T(8,128)(2,1)S(1)} %copy-done.6, ...), custom_call_target="tpu_custom_call" | custom-call | flops 3000000000 | bytes 5242880 | tf_op jit(solution)/shard_map/pallas_call | solution.py:365
  (35 shorter events, 0.4 us)
Async XLA Ops:
  1.8 12.4 %collective-permute-start = (bf16[8,2,8,512]{3,1,0,2:T(2,128)(2,1)S(1)}, bf16[8,2,8,512]{3,1,0,2:T(2,128)(2,1)S(1)}, u32[]{:S(2)}, u32[]{:S(2)}) collective-permute-start(bf16[8,2,8,512]{3,1,0,2:T(2,128)(2,1)S(1)} %get-tuple-element.21), channel_id=1, source_target_pairs={{0,64},{64,128},{128,192},{192,256},{256,320},{320,384},{384,448},... | collective-permute-start | bytes 393224 | tf_op jit(solution)/shard_map/ppermute | solution.py:301
  1.8 5.8 %copy-start.1 = (s32[512,8]{0,1:T(8,128)S(1)}, s32[512,8]{0,1:T(8,128)}, u32[]{:S(2)}) copy-start(s32[512,8]{0,1:T(8,128)} %param.11) | copy-start | bytes 49156
  1.8 5.8 %copy-start.2 = (s32[512]{0:T(512)S(1)}, s32[512]{0:T(512)}, u32[]{:S(2)}) copy-start(s32[512]{0:T(512)} %param.9) | copy-start | bytes 6148
  1.9 5.8 %copy-start.3 = (s32[512]{0:T(512)S(1)}, s32[512]{0:T(512)}, u32[]{:S(2)}) copy-start(s32[512]{0:T(512)} %param.10) | copy-start | bytes 6148
  1.9 5.8 %copy-start.4 = (s32[512]{0:T(512)S(1)}, s32[512]{0:T(512)}, u32[]{:S(2)}) copy-start(s32[512]{0:T(512)} %param.12) | copy-start | bytes 6148
  1.9 12.4 %collective-permute-start.1 = (bf16[8,2,8,512]{3,1,0,2:T(2,128)(2,1)S(1)}, bf16[8,2,8,512]{3,1,0,2:T(2,128)(2,1)S(1)}, u32[]{:S(2)}, u32[]{:S(2)}) collective-permute-start(bf16[8,2,8,512]{3,1,0,2:T(2,128)(2,1)S(1)} %get-tuple-element.20), channel_id=1, source_target_pairs={{64,0},{128,64},{192,128},{256,192},{320,256},{384,320},{448,384},... | collective-permute-start | bytes 393224 | tf_op jit(solution)/shard_map/ppermute | solution.py:302
  90.4 5.2 %copy-start = (f32[512]{0:T(512)S(1)}, f32[512]{0:T(512)}, u32[]{:S(2)}) copy-start(f32[512]{0:T(512)} %param.14) | copy-start | bytes 6148
  90.4 5.4 %copy-start.7 = (bf16[128,2,512]{2,1,0:T(2,128)(2,1)S(1)}, bf16[128,2,512]{2,1,0:T(2,128)(2,1)}, u32[]{:S(2)}) copy-start(bf16[128,2,512]{2,1,0:T(2,128)(2,1)} %param.15) | copy-start | bytes 786436
  90.4 5.4 %copy-start.8 = (f32[512]{0:T(512)S(1)}, f32[512]{0:T(512)}, u32[]{:S(2)}) copy-start(f32[512]{0:T(512)} %param.13) | copy-start | bytes 6148
  90.4 29.3 %all-to-all-start.4 = ((bf16[4,2,2,128,512]{4,3,2,1,0:T(8,128)(2,1)}), bf16[4,2,2,128,512]{4,3,2,1,0:T(8,128)(2,1)S(1)}, u32[]{:S(2)}, u32[]{:S(2)}) async-start(bf16[4,2,2,128,512]{4,3,2,1,0:T(8,128)(2,1)} %bitcast.15), calls=%async_computation.4 | async-start | bytes 4194304 | tf_op jit(solution)/shard_map/all_to_all | solution.py:188
  118.9 0.8 copy-start.5
  119.7 1.0 copy-start.6
